TPU v7x, 32 devices: a whole 2x2x4 slice. The times are simulated.
32 devices in a mesh: rep: 4 (over y, core), shard: 8 (over z, x).
Axes of the slice: x: 2, y: 2, z: 4, core: 2. Of those that a mesh axis runs over, the one named last changes fastest.
Arguments:
- hidden: bfloat16 [14336, 3584], P(('rep', 'shard')), may hold values from -144 to 144
- cotangent: bfloat16 [14336, 1024], P(('rep', 'shard')), may hold values from -6 to 6
- seq_ids: int32 [32, 448], P(('rep', 'shard')), may hold values from 0 to 3, as said below
- response_mask: int32 [32, 448], P(('rep', 'shard')), may hold values from 0 to 1, as said below
- group_ids: int32 [32, 4], P(('rep', 'shard')), may hold values from 0 to 15
- rewards: float32 [32, 4], P(('rep', 'shard')), may hold values from -6 to 6
- new_logp: float32 [32, 448], P(('rep', 'shard')), may hold values from -1.5 to -0.1
- old_logp: float32 [32, 448], P(('rep', 'shard')), may hold values from -1.5 to -0.1
- ref_logp: float32 [32, 448], P(('rep', 'shard')), may hold values from -1.5 to -0.1
- master: float32 [3, 3584, 1024], P(None, 'shard'), may hold values from -6 to 6
Outputs:
- new_master: float32 [3584, 1024], P('shard')
- rollout: bfloat16 [3, 3584, 2048], P(None, None, 'shard')
Inputs may be any that keep to these rules, and one draw needn't show every extreme that they name: `seq_ids`: each row numbers its device's 4 sequences in token order, never falling, each with one token or more. `response_mask`: within a sequence, prompt tokens come before response tokens; a sequence may have no response tokens.
All inputs are finite; a program needn't handle non-finite values.
Results may differ from a plain program's by a relative error of at most 0.0095.
Values may be sent and summed in bfloat16 or wider, within the bound.
A program may use at most 128 MiB of HBM per device.

v0:
```python
import jax
import jax.numpy as jnp
from jax import lax
from jax.sharding import PartitionSpec as P

HEAD = 128
KV_HEADS = 4
TP = 8
SEQ_DEV = 4


def token_coef(seq_row, mask_row, adv_row, new_row, old_row, ref_row):
    onehot = (seq_row[:, None] == jnp.arange(SEQ_DEV, dtype=jnp.int32)[None, :]).astype(jnp.float32)
    maskf = mask_row.astype(jnp.float32)
    lengths = jnp.maximum(jnp.dot(maskf, onehot, precision=lax.Precision.HIGHEST), 1.0)
    tok_len = jnp.dot(onehot, lengths, precision=lax.Precision.HIGHEST)
    tok_adv = jnp.dot(onehot, adv_row, precision=lax.Precision.HIGHEST)
    surrogate = -tok_adv * jnp.exp(new_row - old_row) + 0.2 * (1.0 - jnp.exp(ref_row - new_row))
    return maskf / tok_len * surrogate


def group_advantage(group_flat, reward_flat, stats):
    groups = stats.shape[1]
    onehot = (group_flat[:, None] == jnp.arange(groups, dtype=jnp.int32)[None, :]).astype(
        jnp.float32
    )
    count = jnp.maximum(stats[0], 1.0)
    mean = stats[1] / count
    spread = jnp.sqrt(jnp.maximum(stats[2] / count - mean * mean, 0.0))
    tok_mean = jnp.dot(onehot, mean, precision=lax.Precision.HIGHEST)
    tok_std = jnp.dot(onehot, jnp.maximum(spread, 0.5), precision=lax.Precision.HIGHEST)
    return (reward_flat - tok_mean) / tok_std


def group_sums(group_flat, reward_flat, groups):
    onehot = (group_flat[:, None] == jnp.arange(groups, dtype=jnp.int32)[None, :]).astype(
        jnp.float32
    )
    values = jnp.stack([jnp.ones_like(reward_flat), reward_flat, reward_flat * reward_flat], axis=0)
    return jnp.dot(values, onehot, precision=lax.Precision.HIGHEST)


def rounded(term):
    return lax.optimization_barrier(term.astype(jnp.bfloat16)).astype(jnp.float32)


def rollout_blocks(weights):
    layer_count = weights.shape[0]
    row_count = weights.shape[1]
    paired = weights.reshape(layer_count, row_count, 2, KV_HEADS, HEAD).transpose(0, 1, 3, 2, 4)
    paired = paired.reshape(layer_count, row_count, KV_HEADS, 2 * HEAD)
    by_rank = jnp.repeat(paired, TP // KV_HEADS, axis=2)
    copies = jnp.tile(by_rank, (1, 1, lax.axis_size("shard") // TP, 1))
    return copies.reshape(layer_count, row_count, lax.axis_size("shard") * 2 * HEAD)


def per_device(
    hidden,
    cotangent,
    seq_ids,
    response_mask,
    group_ids,
    rewards,
    new_logp,
    old_logp,
    ref_logp,
    master,
):
    n_rep = lax.axis_size("rep")
    n_shard = lax.axis_size("shard")
    groups = n_rep * n_shard * SEQ_DEV // 8
    rest_cols = lax.all_to_all(
        rollout_blocks(master[1:].astype(jnp.bfloat16)),
        "shard",
        split_axis=2,
        concat_axis=1,
        tiled=True,
    )
    local_sums = group_sums(group_ids[0], rewards[0], groups)
    stats = lax.psum(local_sums, ("rep", "shard"))
    advantage = group_advantage(group_ids[0], rewards[0], stats)
    coef = token_coef(
        seq_ids[0], response_mask[0], advantage, new_logp[0], old_logp[0], ref_logp[0]
    )
    delta = (coef[:, None] * cotangent.astype(jnp.float32)).astype(jnp.bfloat16)
    feature_count = hidden.shape[1]
    partial_value = lax.psum_scatter(
        rounded(
            lax.dot_general(
                hidden, delta, (((0,), (0,)), ((), ())), preferred_element_type=jnp.float32
            )
        ).astype(jnp.bfloat16),
        "shard",
        scatter_dimension=0,
        tiled=True,
    )
    grad = lax.psum(partial_value, "rep").astype(jnp.float32)
    squares = lax.psum(jnp.sum(grad * grad), "shard")
    rms = jnp.sqrt(squares / (feature_count * grad.shape[1]) + 1e-06)
    new_master = master[0] - 0.5 * grad / rms
    first_cols = lax.all_to_all(
        rollout_blocks(new_master[None].astype(jnp.bfloat16)),
        "shard",
        split_axis=2,
        concat_axis=1,
        tiled=True,
    )
    rollout = jnp.concatenate([first_cols, rest_cols], axis=0)
    return (new_master, rollout)


def solution(mesh):
    in_specs = (
        P(("rep", "shard"), None),
        P(("rep", "shard"), None),
        P(("rep", "shard"), None),
        P(("rep", "shard"), None),
        P(("rep", "shard"), None),
        P(("rep", "shard"), None),
        P(("rep", "shard"), None),
        P(("rep", "shard"), None),
        P(("rep", "shard"), None),
        P(None, "shard", None),
    )
    out_specs = (P("shard", None), P(None, None, "shard"))
    return jax.shard_map(
        per_device, mesh=mesh, in_specs=in_specs, out_specs=out_specs, check_vma=False
    )
```

profile of v0, /device:TPU:0, one launch (start us, length us, event | category | flops | bytes accessed | tf_op | source)
XLA Modules:
  0.0 468.4 jit_solution(8274017862780211825)
XLA Ops:
  9.0 41.9 %psum.21 = f32[3,16]{1,0:T(4,128)S(1)} all-reduce(f32[3,16]{1,0:T(4,128)S(1)} %fusion.15), channel_id=1, replica_groups=mesh['rep'=4,'shard'=8] {'rep','shard'}, use_global_device_ids=true, to_apply=%region_0.0 | all-reduce | flops 48 | bytes 384 | tf_op jit(solution)/shard_map/psum | solution.py:80
  55.3 1.0 fusion.11
  57.1 7.5 %fusion = bf16[3584,1024]{0,1:T(8,128)(2,1)} fusion(bf16[448,3584]{1,0:T(8,128)(2,1)S(1)} %copy-done, bf16[448,1024]{1,0:T(8,128)(2,1)} %param.11, f32[448]{0:T(512)S(1)} %add_multiply_fusion), kind=kOutput, calls=%fused_computation.1 | convolution fusion | flops 3293380608 | bytes 11470592 | tf_op jit(solution)/shard_map/dot_general | solution.py:89
  64.6 10.4 %copy.47 = bf16[3584,1024]{1,0:T(8,128)(2,1)} copy(bf16[3584,1024]{0,1:T(8,128)(2,1)} %fusion) | data formatting | bytes 14680064
  75.0 2.3 slice.36
  77.4 2.3 reshape.41
  79.6 5.7 %copy.49 = bf16[2,448,2,4,128]{1,0,4,2,3:T(2,128)(2,1)S(1)} copy(bf16[2,448,2,4,128]{4,3,2,1,0:T(4,128)(2,1)} %reshape.41) | data formatting | bytes 3670016 | tf_op jit(solution)/shard_map/transpose | solution.py:50
  85.3 4.2 broadcast_in_dim.15
  89.5 5.3 %all-to-all-start.1 = ((bf16[2,448,2048]{1,0,2:T(2,128)(2,1)}), bf16[2,448,2048]{1,0,2:T(2,128)(2,1)}, u32[]{:S(2)}, u32[]{:S(2)}) async-start(bf16[2,448,2048]{1,0,2:T(2,128)(2,1)} %bitcast.83), calls=%async_computation.1 | async-start | bytes 8388608 | tf_op jit(solution)/shard_map/all_to_all | solution.py:72
  94.9 188.3 %reduce-scatter.4.cloned.1.call-done = bf16[448,1024]{1,0:T(8,128)(2,1)} async-done(((bf16[3584,1024]{1,0:T(8,128)(2,1)}), bf16[448,1024]{1,0:T(8,128)(2,1)}) %reduce-scatter.4.cloned.1.call-update) | async-done | bytes 917520
  283.2 2.2 copy.48
  285.4 36.1 %all-reduce.2.cloned.1.call-done = bf16[448,1024]{0,1:T(8,128)(2,1)} async-done(((bf16[448,1024]{0,1:T(8,128)(2,1)}), bf16[448,1024]{0,1:T(8,128)(2,1)}) %all-reduce.2.cloned.1.call-update) | async-done | bytes 917520 | tf_op jit(solution)/shard_map/psum | solution.py:97
  321.5 2.4 fusion.3
  323.9 1.9 copy.51
  325.7 22.1 %psum.23 = f32[]{:T(128)} all-reduce(f32[]{:T(128)} %fusion.3), channel_id=1, replica_groups=mesh['rep'=4,'shard'=8] {'shard'}, use_global_device_ids=true, to_apply=%region_4.0 | all-reduce | flops 1 | bytes 8 | tf_op jit(solution)/shard_map/psum | solution.py:98
  348.6 3.0 fusion.36
  351.6 3.6 copy.33
  355.2 2.7 reshape.40
  358.6 2.5 broadcast_in_dim.6
  361.1 5.3 %broadcast_in_dim.14 = bf16[1,448,2048]{2,1,0:T(8,128)(2,1)} reshape(bf16[448,4,2,256]{3,2,1,0:T(2,128)(2,1)} %broadcast_in_dim.6) | data formatting | bytes 3670016 | tf_op jit(solution)/shard_map/broadcast_in_dim | solution.py:52
  366.4 10.7 %copy.35 = bf16[1,448,2048]{1,0,2:T(2,128)(2,1)} copy(bf16[1,448,2048]{2,1,0:T(8,128)(2,1)} %broadcast_in_dim.14) | data formatting | bytes 3670016 | tf_op jit(solution)/shard_map/broadcast_in_dim | solution.py:52
  377.6 15.4 %reduce = bf16[2048,448]{1,0:T(8,128)(2,1)} reduce(bf16[2048,1,448]{2,1,0:T(2,128)(2,1)} %bitcast.84, bf16[]{:T(256)} %broadcast.50), dimensions={1}, to_apply=%bitcast.77.reduce_sub_computation | reduce | bytes 3670018
  393.1 6.8 %reshape.57 = bf16[8,2,57344]{2,1,0:T(2,128)(2,1)} reshape(bf16[2048,448]{1,0:T(8,128)(2,1)} %reduce) | data formatting | bytes 3670016
  399.8 4.3 all-to-all-start
  404.2 11.1 %copy.46 = bf16[2,448,8,256]{3,1,2,0:T(8,128)(2,1)} copy(bf16[2,448,8,256]{1,0,3,2:T(2,128)(2,1)} %bitcast.27) | data formatting | bytes 7340032 | tf_op jit(solution)/shard_map/all_to_all | solution.py:72
  415.3 1.7 copy.42
  417.0 25.9 %all-to-all-done = bf16[8,2,57344]{2,1,0:T(2,128)(2,1)} async-done(((bf16[8,2,57344]{2,1,0:T(2,128)(2,1)}), bf16[8,2,57344]{2,1,0:T(2,128)(2,1)}, u32[]{:S(2)}, u32[]{:S(2)}) %all-to-all-start) | async-done | bytes 1835040 | tf_op jit(solution)/shard_map/all_to_all | solution.py:101
  442.9 7.2 %reshape.58 = bf16[2048,1,448]{2,1,0:T(2,128)(2,1)} reshape(bf16[8,2,57344]{2,1,0:T(2,128)(2,1)} %all-to-all-done) | data formatting | bytes 3670016
  450.1 2.8 copy.50
  452.9 3.0 copy.43
  455.8 2.0 copy.37
  458.4 2.9 pad_maximum_fusion
  (28 shorter events, 9.0 us)
Async XLA Ops:
  7.2 49.9 %copy-start = (bf16[448,3584]{1,0:T(8,128)(2,1)S(1)}, bf16[448,3584]{1,0:T(8,128)(2,1)}, u32[]{:S(2)}) copy-start(bf16[448,3584]{1,0:T(8,128)(2,1)} %param.10) | copy-start | bytes 9633796
  7.2 276.0 %reduce-scatter.4.cloned.1.call-start = ((), (), s32[]{:S(2)}) async-start(), calls=%async_computation.4 | async-start | bytes 8257536
  89.5 310.4 %all-to-all-start.1 = ((bf16[2,448,2048]{1,0,2:T(2,128)(2,1)}), bf16[2,448,2048]{1,0,2:T(2,128)(2,1)}, u32[]{:S(2)}, u32[]{:S(2)}) async-start(bf16[2,448,2048]{1,0,2:T(2,128)(2,1)} %bitcast.83), calls=%async_computation.1 | async-start | bytes 8388608 | tf_op jit(solution)/shard_map/all_to_all | solution.py:72
  94.8 226.7 %all-reduce.2.cloned.1.call-start = ((), (), s32[]{:S(2)}) async-start(), calls=%async_computation.3 | async-start | bytes 2097152 | tf_op jit(solution)/shard_map/psum | solution.py:97
  285.4 38.5 %slice-start = ((f32[3,448,1024]{2,1,0:T(8,128)}), f32[1,448,1024]{2,1,0:T(8,128)S(1)}, s32[]{:S(2)}) async-start(f32[3,448,1024]{2,1,0:T(8,128)} %param.19), calls=%async_computation.5 | async-start | bytes 3670016 | tf_op jit(solution)/shard_map/slice | solution.py:100
  323.9 24.7 %copy-start.3 = (bf16[448,1024]{0,1:T(8,128)(2,1)S(1)}, bf16[448,1024]{0,1:T(8,128)(2,1)}, u32[]{:S(2)}) copy-start(bf16[448,1024]{0,1:T(8,128)(2,1)} %all-reduce.2.cloned.1.call-done) | copy-start | bytes 2752516
  399.8 43.1 %all-to-all-start = ((bf16[8,2,57344]{2,1,0:T(2,128)(2,1)}), bf16[8,2,57344]{2,1,0:T(2,128)(2,1)}, u32[]{:S(2)}, u32[]{:S(2)}) async-start(bf16[8,2,57344]{2,1,0:T(2,128)(2,1)} %reshape.57), calls=%async_computation | async-start | bytes 3670016 | tf_op jit(solution)/shard_map/all_to_all | solution.py:101
  455.8 2.6 copy-start.2
  458.4 3.1 copy-start.1
Sparse Core Ops, SparseCore 0:
  75.2 207.9 reduce-scatter.3
  286.1 35.3 all-reduce.1
where the time goes:
time: 470 us; the launch traced here: 468 us
  waiting for transfers between devices  250 us (53%)
  local copies, waits for them, and re-layouts  90.3 us (19%)
  blocking collectives  64.1 us (14%)
  other arithmetic  26 us (6%)
  between operations  14.8 us (3%)
  matrix products  13.1 us (3%)
  starting transfers between devices  9.74 us (2%)
    unnamed x3, waiting for transfers between devices  188 us
    psum x1, blocking collectives, per_device(): stats = lax.psum(local_sums, ('rep', 'shard'))  41.9 us
    psum x1, waiting for transfers between devices, per_device(): grad = lax.psum(partial_value, 'rep').astype(jnp.float32)  36.1 us
    unnamed x16, local copies, waits for them, and re-layouts  34.2 us
    all_to_all x1, waiting for transfers between devices, per_device(): lax.all_to_all(rollout_blocks(new_master[None].astype(jnp.bfloat16)), 'sh...  25.9 us
    broadcast_in_dim x4, local copies, waits for them, and re-layouts, rollout_blocks(): by_rank = jnp.repeat(paired, TP // KV_HEADS, axis=2)  22.7 us
    psum x1, blocking collectives, per_device(): squares = lax.psum(jnp.sum(grad * grad), 'shard')  22.1 us
    unnamed x1, other arithmetic  15.4 us
  transfers between devices with their start and end apart: 4, of which 3 were waited for; matrix products, arithmetic and copies ran while one was open for 18% of the time, Pallas kernels for 0%

commit v1 on v0

--- a/solution.py
+++ b/solution.py
@@ -1,3 +1,4 @@
+import functools
 import jax
 import jax.numpy as jnp
 from jax import lax
@@ -7,6 +8,13 @@
 KV_HEADS = 4
 TP = 8
 SEQ_DEV = 4
+
+
+def _watch_row(inputs, lane_axis):
+    return jax.lax.all_gather(inputs, lane_axis).sum(axis=0)
+
+
+unite_circles = functools.partial(_watch_row, lane_axis="rep")
 
 
 def token_coef(seq_row, mask_row, adv_row, new_row, old_row, ref_row):
@@ -94,7 +102,7 @@
         scatter_dimension=0,
         tiled=True,
     )
-    grad = lax.psum(partial_value, "rep").astype(jnp.float32)
+    grad = unite_circles(partial_value).astype(jnp.float32)
     squares = lax.psum(jnp.sum(grad * grad), "shard")
     rms = jnp.sqrt(squares / (feature_count * grad.shape[1]) + 1e-06)
     new_master = master[0] - 0.5 * grad / rms

time: 470 us -> 448 us (0.953)
  local copies, waits for them, and re-layouts: 90.3 us -> 71.1 us
    reduce_scatter x0 -> x1, waiting for transfers between devices: none -> 188 us  [per_device(): lax.psum_scatter(rounded(lax.dot_general(hidden, delta, (((0,), (0,)), ((...]
    unnamed x3 -> x2, waiting for transfers between devices: 188 us -> 0.03 us
    psum x1 -> x0, waiting for transfers between devices: 36.1 us -> none  [per_device(): grad = lax.psum(partial_value, 'rep').astype(jnp.float32)]
    all_gather x0 -> x1, waiting for transfers between devices: none -> 32.1 us  [_watch_row(): return jax.lax.all_gather(inputs, lane_axis).sum(axis=0)]
    unnamed x16 -> x11, local copies, waits for them, and re-layouts: 34.2 us -> 23.7 us
  transfers between devices with their start and end apart: 4 -> 4, of which waited for: 3 -> 3; matrix products, arithmetic and copies ran while one was open for 18% -> 16% of each run, Pallas kernels for 0% -> 0%
where the time goes in v1:
time: 448 us; the launch traced here: 446 us
  waiting for transfers between devices  246 us (55%)
  local copies, waits for them, and re-layouts  71.1 us (16%)
  blocking collectives  64.1 us (14%)
  other arithmetic  28.3 us (6%)
  between operations  14.9 us (3%)
  matrix products  13.2 us (3%)
  starting transfers between devices  9.02 us (2%)
    reduce_scatter x1, waiting for transfers between devices, per_device(): lax.psum_scatter(rounded(lax.dot_general(hidden, delta, (((0,), (0,)), ((...  188 us
    psum x1, blocking collectives, per_device(): stats = lax.psum(local_sums, ('rep', 'shard'))  41.9 us
    all_gather x1, waiting for transfers between devices, _watch_row(): return jax.lax.all_gather(inputs, lane_axis).sum(axis=0)  32.1 us
    all_to_all x1, waiting for transfers between devices, per_device(): lax.all_to_all(rollout_blocks(new_master[None].astype(jnp.bfloat16)), 'sh...  25.4 us
    unnamed x11, local copies, waits for them, and re-layouts  23.7 us
    psum x1, blocking collectives, per_device(): squares = lax.psum(jnp.sum(grad * grad), 'shard')  22.1 us
    broadcast_in_dim x4, local copies, waits for them, and re-layouts, rollout_blocks(): by_rank = jnp.repeat(paired, TP // KV_HEADS, axis=2)  18.4 us
    unnamed x1, other arithmetic  14.1 us
  transfers between devices with their start and end apart: 4, of which 3 were waited for; matrix products, arithmetic and copies ran while one was open for 16% of the time, Pallas kernels for 0%

profile of v1, /device:TPU:0, one launch (start us, length us, event | category | flops | bytes accessed | tf_op | source)
XLA Modules:
  0.0 446.5 jit_solution(1976028733505066821)
XLA Ops:
  8.1 1.0 fusion.15
  9.0 41.9 %psum.14 = f32[3,16]{1,0:T(4,128)S(1)} all-reduce(f32[3,16]{1,0:T(4,128)S(1)} %fusion.15), channel_id=1, replica_groups=mesh['rep'=4,'shard'=8] {'rep','shard'}, use_global_device_ids=true, to_apply=%region_0.0 | all-reduce | flops 48 | bytes 384 | tf_op jit(solution)/shard_map/psum | solution.py:88
  53.4 0.9 fusion.5
  54.3 1.0 fusion.10
  55.3 1.0 fusion.11
  57.1 7.5 %fusion = bf16[3584,1024]{0,1:T(8,128)(2,1)} fusion(bf16[448,3584]{1,0:T(8,128)(2,1)S(1)} %copy-done, bf16[448,1024]{1,0:T(8,128)(2,1)} %param.11, f32[448]{0:T(512)S(1)} %add_multiply_fusion), kind=kOutput, calls=%fused_computation.1 | convolution fusion | flops 3293380608 | bytes 11470592 | tf_op jit(solution)/shard_map/dot_general | solution.py:97
  64.7 10.4 %copy.35 = bf16[3584,1024]{1,0:T(8,128)(2,1)} copy(bf16[3584,1024]{0,1:T(8,128)(2,1)} %fusion) | data formatting | bytes 14680064
  75.1 2.3 slice.38
  77.4 2.3 reshape.58
  79.7 5.7 %copy.37 = bf16[2,448,2,4,128]{1,0,4,2,3:T(2,128)(2,1)S(1)} copy(bf16[2,448,2,4,128]{4,3,2,1,0:T(4,128)(2,1)} %reshape.58) | data formatting | bytes 3670016 | tf_op jit(solution)/shard_map/transpose | solution.py:58
  85.3 4.2 broadcast_in_dim.15
  89.5 5.3 %all-to-all-start.1 = ((bf16[2,448,2048]{1,0,2:T(2,128)(2,1)}), bf16[2,448,2048]{1,0,2:T(2,128)(2,1)}, u32[]{:S(2)}, u32[]{:S(2)}) async-start(bf16[2,448,2048]{1,0,2:T(2,128)(2,1)} %bitcast.88), calls=%async_computation.1 | async-start | bytes 8388608 | tf_op jit(solution)/shard_map/all_to_all | solution.py:80
  94.9 188.3 %reduce-scatter.4.cloned.1.call-done = bf16[448,1024]{1,0:T(8,128)(2,1)} async-done(((bf16[3584,1024]{1,0:T(8,128)(2,1)}), bf16[448,1024]{1,0:T(8,128)(2,1)}) %reduce-scatter.4.cloned.1.call-update) | async-done | bytes 917520 | tf_op jit(solution)/shard_map/reduce_scatter | solution.py:95
  283.3 32.1 %all-gather.3.cloned.1.call-done = bf16[1792,1024]{1,0:T(8,128)(2,1)} async-done(((bf16[448,1024]{1,0:T(8,128)(2,1)}), bf16[1792,1024]{1,0:T(8,128)(2,1)}) %all-gather.3.cloned.1.call-update) | async-done | bytes 3670032 | tf_op jit(solution)/shard_map/all_gather | solution.py:14
  315.4 2.9 reduce_sum.21
  318.3 1.1 fusion.2
  319.4 22.1 %psum.15 = f32[]{:T(128)} all-reduce(f32[]{:T(128)} %fusion.2), channel_id=1, replica_groups=mesh['rep'=4,'shard'=8] {'shard'}, use_global_device_ids=true, to_apply=%region_4.0 | all-reduce | flops 1 | bytes 8 | tf_op jit(solution)/shard_map/psum | solution.py:106
  342.2 1.8 fusion.3
  346.8 1.3 broadcast_in_dim.6
  348.1 2.3 broadcast_in_dim.14
  350.4 10.7 %copy.24 = bf16[1,448,2048]{1,0,2:T(2,128)(2,1)} copy(bf16[1,448,2048]{2,1,0:T(8,128)(2,1)} %broadcast_in_dim.14) | data formatting | bytes 3670016 | tf_op jit(solution)/shard_map/broadcast_in_dim | solution.py:60
  361.6 14.1 %reduce.1 = bf16[2048,448]{1,0:T(8,128)(2,1)S(1)} reduce(bf16[2048,1,448]{2,1,0:T(2,128)(2,1)} %bitcast.89, bf16[]{:T(256)} %broadcast.68), dimensions={1}, to_apply=%bitcast.82.reduce_sub_computation | reduce | bytes 3670018
  375.7 4.4 reshape.75
  380.1 3.6 all-to-all-start
  383.7 11.1 %copy.34 = bf16[2,448,8,256]{3,1,2,0:T(8,128)(2,1)} copy(bf16[2,448,8,256]{1,0,3,2:T(2,128)(2,1)} %bitcast.28) | data formatting | bytes 7340032 | tf_op jit(solution)/shard_map/all_to_all | solution.py:80
  394.9 3.2 bitcast_subtract_fusion.1
  398.0 25.4 %all-to-all-done = bf16[8,2,57344]{2,1,0:T(2,128)(2,1)S(1)} async-done(((bf16[8,2,57344]{2,1,0:T(2,128)(2,1)}), bf16[8,2,57344]{2,1,0:T(2,128)(2,1)S(1)}, u32[]{:S(2)}, u32[]{:S(2)}) %all-to-all-start) | async-done | bytes 1835040 | tf_op jit(solution)/shard_map/all_to_all | solution.py:109
  423.4 4.8 %reshape.76 = bf16[2048,1,448]{2,1,0:T(2,128)(2,1)} reshape(bf16[8,2,57344]{2,1,0:T(2,128)(2,1)S(1)} %all-to-all-done) | data formatting | bytes 3670016
  428.2 2.8 copy.38
  431.0 3.0 copy.31
  434.0 2.0 copy.26
  436.6 2.9 pad_maximum_fusion
  (24 shorter events, 8.1 us)
Async XLA Ops:
  7.2 49.9 %copy-start = (bf16[448,3584]{1,0:T(8,128)(2,1)S(1)}, bf16[448,3584]{1,0:T(8,128)(2,1)}, u32[]{:S(2)}) copy-start(bf16[448,3584]{1,0:T(8,128)(2,1)} %param.10) | copy-start | bytes 9633796
  7.2 276.1 %reduce-scatter.4.cloned.1.call-start = ((), (), s32[]{:S(2)}) async-start(), calls=%async_computation.4 | async-start | bytes 8257536 | tf_op jit(solution)/shard_map/reduce_scatter | solution.py:95
  89.5 290.6 %all-to-all-start.1 = ((bf16[2,448,2048]{1,0,2:T(2,128)(2,1)}), bf16[2,448,2048]{1,0,2:T(2,128)(2,1)}, u32[]{:S(2)}, u32[]{:S(2)}) async-start(bf16[2,448,2048]{1,0,2:T(2,128)(2,1)} %bitcast.88), calls=%async_computation.1 | async-start | bytes 8388608 | tf_op jit(solution)/shard_map/all_to_all | solution.py:80
  94.9 220.5 %all-gather.3.cloned.1.call-start = ((), (), s32[]{:S(2)}) async-start(), calls=%async_computation.3 | async-start | bytes 4587520 | tf_op jit(solution)/shard_map/all_gather | solution.py:14
  380.1 43.3 %all-to-all-start = ((bf16[8,2,57344]{2,1,0:T(2,128)(2,1)}), bf16[8,2,57344]{2,1,0:T(2,128)(2,1)S(1)}, u32[]{:S(2)}, u32[]{:S(2)}) async-start(bf16[8,2,57344]{2,1,0:T(2,128)(2,1)} %reshape.75), calls=%async_computation | async-start | bytes 3670016 | tf_op jit(solution)/shard_map/all_to_all | solution.py:109
  434.0 2.6 copy-start.2
  436.6 3.1 copy-start.1
Sparse Core Ops, SparseCore 0:
  75.2 207.9 reduce-scatter.3
  284.8 30.5 all-gather.2
